TPU v7x, 32 devices: a whole 2x2x4 slice. The times are simulated.
32 devices in a mesh: dp: 8 (over y, x, core), tensor: 4 (over z).
Axes of the slice: x: 2, y: 2, z: 4, core: 2. Of those that a mesh axis runs over, the one named last changes fastest.
Arguments:
- tokens: bfloat16 [128, 5376], P('dp'), may hold values from -6 to 6
- lengths: int32 [128], P('dp'), may hold values from 1 to 1024, as said below
- positions: int32 [128], P('dp'), may hold values from 1 to 33791, as said below
- in_gain: float32 [5376], replicated, may hold values from 0.25 to 1.75
- q_weight: bfloat16 [5376, 4096], P('dp', 'tensor'), may hold values from -0.078125 to 0.078125
- k_weight: bfloat16 [5376, 2048], P('dp', 'tensor'), may hold values from -0.078125 to 0.078125
- v_weight: bfloat16 [5376, 2048], P('dp', 'tensor'), may hold values from -0.078125 to 0.078125
- q_gain: float32 [128], replicated, may hold values from 0.1 to 1.9
- k_gain: float32 [128], replicated, may hold values from 0.1 to 1.9
- key_cache: bfloat16 [128, 1024, 2048], P('dp', None, 'tensor'), may hold values from -480 to 480
- value_cache: bfloat16 [128, 1024, 2048], P('dp', None, 'tensor'), may hold values from -6 to 6
- out_weight: bfloat16 [4096, 5376], P('tensor', 'dp'), may hold values from -0.09375 to 0.09375
- post_gain: float32 [5376], replicated, may hold values from 0.25 to 1.75
Outputs:
- hidden_out: bfloat16 [128, 5376], P('dp')
- new_keys: bfloat16 [128, 2048], P('dp', 'tensor')
- new_values: bfloat16 [128, 2048], P('dp', 'tensor')
Inputs may be any that keep to these rules, and one draw needn't show every extreme that they name: Slots 0 to lengths - 1 of a sequence hold its cache; some sequence has exactly 1024. `positions`: each position is at least the sequence's length.
All inputs are finite; a program needn't handle non-finite values.
Results may differ from a plain program's by a relative error of at most 0.012.
The roundings to bfloat16 on the way count: a program that leaves them out, or rounds other values in their place, can miss the bound.
Values may be sent and summed in bfloat16 or wider, within the bound.
A program may use at most 64 MiB of HBM per device.

v0:
```python
import jax
import jax.numpy as jnp
from jax import lax
from jax.sharding import PartitionSpec as P

HD = 128
QPRE = 168
epsilon = 1e-06
rope_base = 1000000.0
rope_factor = 8.0


def rms_scale(vectors, gain):
    mean_square = jnp.mean(vectors * vectors, axis=-1, keepdims=True)
    return vectors * lax.rsqrt(mean_square + epsilon) * gain


def rotate(vectors, positions):
    half_width = vectors.shape[-1] // 2
    exponent = jnp.arange(half_width, dtype=jnp.float32) * (2.0 / vectors.shape[-1])
    frequency = jnp.power(rope_base, -exponent)
    angles = (positions.astype(jnp.float32) / rope_factor)[:, None] * frequency[None, :]
    cos_part = jnp.cos(angles)[:, None, :]
    sin_part = jnp.sin(angles)[:, None, :]
    first_half = vectors[..., :half_width]
    second_half = vectors[..., half_width:]
    return jnp.concatenate(
        [
            first_half * cos_part - second_half * sin_part,
            second_half * cos_part + first_half * sin_part,
        ],
        axis=-1,
    )


def per_device(
    tokens,
    lengths,
    positions,
    in_gain,
    q_weight,
    k_weight,
    v_weight,
    q_gain,
    k_gain,
    key_cache,
    value_cache,
    out_weight,
    post_gain,
):
    tok_rows = tokens.shape[0]
    q_cols = q_weight.shape[1]
    kv_cols = k_weight.shape[1]
    local_heads = q_cols // HD
    local_kv = kv_cols // HD
    per_group = local_heads // local_kv
    cache_len = key_cache.shape[1]
    normed = rms_scale(tokens.astype(jnp.float32), in_gain).astype(jnp.bfloat16)
    spread = lax.all_to_all(normed, "dp", split_axis=1, concat_axis=0, tiled=True)
    joined = lax.psum_scatter(
        jnp.concatenate(
            [
                jnp.dot(spread, q_weight, preferred_element_type=jnp.float32),
                jnp.dot(spread, k_weight, preferred_element_type=jnp.float32),
                jnp.dot(spread, v_weight, preferred_element_type=jnp.float32),
            ],
            axis=1,
        ),
        "dp",
        scatter_dimension=0,
        tiled=True,
    )
    q_raw = joined[:, :q_cols]
    k_raw = joined[:, q_cols : q_cols + kv_cols]
    v_raw = joined[:, q_cols + kv_cols :]
    new_values = v_raw.astype(jnp.bfloat16)
    queries = (
        rotate(rms_scale(q_raw.reshape(tok_rows, local_heads, HD), q_gain), positions)
        * QPRE ** (-0.5)
    ).astype(jnp.bfloat16)
    new_keys = (
        rotate(rms_scale(k_raw.reshape(tok_rows, local_kv, HD), k_gain), positions)
        .astype(jnp.bfloat16)
        .reshape(tok_rows, kv_cols)
    )
    grouped = queries.reshape(tok_rows, local_kv, per_group, HD)
    cache_keys = key_cache.reshape(tok_rows, cache_len, local_kv, HD)
    cache_values = value_cache.reshape(tok_rows, cache_len, local_kv, HD)
    self_score = jnp.einsum(
        "bgrd,bgd->bgr",
        grouped,
        new_keys.reshape(tok_rows, local_kv, HD),
        preferred_element_type=jnp.float32,
    )
    self_values = new_values.reshape(tok_rows, local_kv, HD).astype(jnp.float32)
    scores = jnp.einsum("bgrd,bjgd->bgrj", grouped, cache_keys, preferred_element_type=jnp.float32)
    usable = jnp.arange(cache_len)[None, :] < lengths[:, None]
    scores = jnp.where(usable[:, None, None, :], scores, -jnp.inf)
    largest = jnp.maximum(jnp.max(scores, axis=-1), self_score)
    weights = jnp.exp(scores - largest[..., None])
    self_weight = jnp.exp(self_score - largest)
    running = jnp.sum(weights, axis=-1) + self_weight
    rounded_self = lax.optimization_barrier(self_weight.astype(jnp.bfloat16)).astype(jnp.float32)
    mixture = jnp.einsum(
        "bgrj,bjgd->bgrd",
        weights.astype(jnp.bfloat16),
        cache_values,
        preferred_element_type=jnp.float32,
    )
    mixture = mixture + rounded_self[..., None] * self_values[:, :, None, :]
    attended = (mixture / running[..., None]).reshape(tok_rows, q_cols).astype(jnp.bfloat16)
    products = jnp.dot(
        lax.all_gather(attended, "dp", axis=0, tiled=True),
        out_weight,
        preferred_element_type=jnp.float32,
    )
    partial_value = lax.all_to_all(products, "dp", split_axis=0, concat_axis=1, tiled=True)
    summed = lax.psum(partial_value, "tensor")
    hidden_out = (tokens.astype(jnp.float32) + rms_scale(summed, post_gain)).astype(jnp.bfloat16)
    return (hidden_out, new_keys, new_values)


def solution(mesh):
    return jax.shard_map(
        per_device,
        mesh=mesh,
        in_specs=(
            P("dp", None),
            P("dp"),
            P("dp"),
            P(),
            P("dp", "tensor"),
            P("dp", "tensor"),
            P("dp", "tensor"),
            P(),
            P(),
            P("dp", None, "tensor"),
            P("dp", None, "tensor"),
            P("tensor", "dp"),
            P(),
        ),
        out_specs=(P("dp", None), P("dp", "tensor"), P("dp", "tensor")),
        check_vma=False,
    )
```

profile of v0, /device:TPU:0, one launch (start us, length us, event | category | flops | bytes accessed | tf_op | source)
XLA Modules:
  0.0 155.1 jit_solution(9750821802335823185)
XLA Ops:
  7.2 1.2 fusion.18
  8.4 1.0 fusion.20
  9.8 11.2 %all_to_all.38 = bf16[16,8,672]{2,0,1:T(8,128)(2,1)S(1)} all-to-all(bf16[16,8,672]{2,0,1:T(8,128)(2,1)S(1)} %copy.23), channel_id=1, replica_groups=mesh['dp'=8,'tensor'=4] {'dp'}, dimensions={1} | all-to-all | bytes 344064 | tf_op jit(solution)/shard_map/all_to_all | solution.py:59
  21.4 1.4 fusion.33
  22.8 1.4 fusion.34
  24.2 1.1 pad_maximum_fusion
  25.3 0.7 convert_multiply_fusion.2
  26.0 0.7 iota_compare_fusion
  26.8 33.9 %reduce-scatter.2.cloned.1.call-done = f32[16,2048]{1,0:T(8,128)} async-done(((f32[128,2048]{1,0:T(8,128)}), f32[16,2048]{1,0:T(8,128)}) %reduce-scatter.2.cloned.1.call-update) | async-done | bytes 131088 | tf_op jit(solution)/shard_map/reduce_scatter | solution.py:60
  60.7 0.8 slice.32
  61.6 0.8 slice_bitcast_fusion
  62.6 0.7 multiply_multiply_fusion.1
  63.3 0.7 multiply_multiply_fusion
  64.7 11.0 %fusion.31 = (f32[16,4,2]{2,1,0:T(4,128)}, f32[16,4,2,1024]{3,2,1,0:T(2,128)S(1)}) fusion(bf16[16,4,2,128]{3,2,1,0:T(2,128)(2,1)S(1)} %fusion.26, pred[16,1024]{1,0:T(8,128)(4,1)S(1)} %iota_compare_fusion, bf16[16,1024,512]{2,1,0:T(8,128)(2,1)} %param.22), kind=kOutput, calls=%fused_computation.51 | convolution fusion | flops 33816448 | bytes 17351168 | tf_op jit(solution)/shard_map/bgrd,bjgd->bgrj/dot_general | solution.py:96
  75.7 0.8 fusion.30
  77.2 1.4 slice.46
  78.5 1.3 reshape.151
  80.4 7.3 %fusion.12 = bf16[16,4,2,128]{3,2,1,0:T(2,128)(2,1)S(1)} fusion(f32[16,4,2,1024]{3,2,1,0:T(2,128)S(1)} %get-tuple-element.12, f32[16,4,2]{2,1,0:T(4,128)S(1)} %get-tuple-element.4, f32[16,4,2]{2,1,0:T(4,128)S(1)} %bitcast.70, f32[16,4,128]{2,1,0:T(4,128)} %reshape.151, f32[16,4,2]{2,1,0:T(4,128)} %convert_element_type.58, bf16[16,1024,512]{2,1,0:T(8,128)(2,1)} %param.23), kind=kOutput, calls=%fused_computation.9 | convolution fusion | flops 33882112 | bytes 17368576 | tf_op jit(solution)/shard_map/bgrj,bjgd->bgrd/dot_general | solution.py:104
  87.7 9.2 %all_gather.3 = bf16[128,1024]{1,0:T(8,128)(2,1)S(1)} all-gather(bf16[16,1024]{1,0:T(8,128)(2,1)S(1)} %convert_element_type.62), channel_id=1, replica_groups=mesh['dp'=8,'tensor'=4] {'dp'}, dimensions={0}, use_global_device_ids=true | all-gather | bytes 294912 | tf_op jit(solution)/shard_map/all_gather | solution.py:113
  97.6 10.8 %all_to_all.39 = f32[8,16,672]{2,1,0:T(8,128)S(1)} all-to-all(f32[8,16,672]{2,1,0:T(8,128)S(1)} %bitcast.61), channel_id=1, replica_groups=mesh['dp'=8,'tensor'=4] {'dp'}, dimensions={0} | all-to-all | bytes 688128 | tf_op jit(solution)/shard_map/all_to_all | solution.py:117
  108.6 0.9 all_to_all.35
  110.3 35.1 %all-reduce.2.cloned.1.call-done = f32[16,5376]{1,0:T(8,128)} async-done(((f32[16,5376]{1,0:T(8,128)}), f32[16,5376]{1,0:T(8,128)}) %all-reduce.2.cloned.1.call-update) | async-done | bytes 344080 | tf_op jit(solution)/shard_map/psum | solution.py:118
  145.4 1.1 multiply_reduce_fusion
  146.5 1.8 %fusion.21 = bf16[16,5376]{1,0:T(8,128)(2,1)} fusion(bf16[16,5376]{1,0:T(8,128)(2,1)S(1)} %copy-done.1, f32[16,5376]{1,0:T(8,128)} %all-reduce.2.cloned.1.call-done, f32[5376]{0:T(1024)} %param.25, f32[16]{0:T(128)S(1)} %add_rsqrt_fusion.2), kind=kLoop, calls=%fused_computation.18 | loop fusion | flops 430080 | bytes 709696 | tf_op jit(solution)/shard_map/convert_element_type | solution.py:119
  (36 shorter events, 4.5 us)
Async XLA Ops:
  7.2 13.9 %copy-start = (bf16[672,1024]{1,0:T(8,128)(2,1)S(1)}, bf16[672,1024]{1,0:T(8,128)(2,1)}, u32[]{:S(2)}) copy-start(bf16[672,1024]{1,0:T(8,128)(2,1)} %param.17) | copy-start | bytes 4128772
  7.2 53.5 %reduce-scatter.2.cloned.1.call-start = ((), (), s32[]{:S(2)}) async-start(), calls=%async_computation.3 | async-start | bytes 1179648 | tf_op jit(solution)/shard_map/reduce_scatter | solution.py:60
  25.3 120.1 %all-reduce.2.cloned.1.call-start = ((), (), s32[]{:S(2)}) async-start(), calls=%async_computation.4 | async-start | bytes 688128 | tf_op jit(solution)/shard_map/psum | solution.py:118
  64.7 32.3 %copy-start.2 = (bf16[1024,672]{0,1:T(8,128)(2,1)S(1)}, bf16[1024,672]{0,1:T(8,128)(2,1)}, u32[]{:S(2)}) copy-start(bf16[1024,672]{0,1:T(8,128)(2,1)} %param.24) | copy-start | bytes 4128772
  75.7 70.8 %copy-start.1 = (bf16[16,5376]{1,0:T(8,128)(2,1)S(1)}, bf16[16,5376]{1,0:T(8,128)(2,1)}, u32[]{:S(2)}) copy-start(bf16[16,5376]{1,0:T(8,128)(2,1)} %param.13) | copy-start | bytes 516100
Sparse Core Ops, SparseCore 0:
  25.4 35.3 reduce-scatter.1
  109.7 35.6 all-reduce.1
where the time goes:
time: 156 us; the launch traced here: 155 us
  waiting for transfers between devices  69 us (44%)
  blocking collectives  31.3 us (20%)
  matrix products  22.2 us (14%)
  between operations  14.2 us (9%)
  other arithmetic  11.8 us (8%)
  local copies, waits for them, and re-layouts  6.5 us (4%)
    psum x1, waiting for transfers between devices, per_device(): summed = lax.psum(partial_value, 'tensor')  35.1 us
    reduce_scatter x1, waiting for transfers between devices, per_device(): lax.psum_scatter(jnp.concatenate([jnp.dot(spread, q_weight, preferred_ele...  33.9 us
    all_to_all x1, blocking collectives, per_device(): lax.all_to_all(normed, 'dp', split_axis=1, concat_axis=0, tiled=True)  11.2 us
    dot_general x1, matrix products, per_device(): jnp.einsum('bgrd,bjgd->bgrj', grouped, cache_keys, preferred_element_type...  11 us
    all_to_all x1, blocking collectives, per_device(): lax.all_to_all(products, 'dp', split_axis=0, concat_axis=1, tiled=True)  10.8 us
    all_gather x1, blocking collectives, per_device(): lax.all_gather(attended, 'dp', axis=0, tiled=True)  9.25 us
    dot_general x1, matrix products, per_device(): jnp.einsum('bgrj,bjgd->bgrd', weights.astype(jnp.bfloat16), cache_values,...  7.27 us
  transfers between devices with their start and end apart: 2, of which 2 were waited for; matrix products, arithmetic and copies ran while one was open for 1% of the time, Pallas kernels for 0%

commit v1 on v0

--- a/solution.py
+++ b/solution.py
@@ -114,7 +114,15 @@
         out_weight,
         preferred_element_type=jnp.float32,
     )
-    partial_value = lax.all_to_all(products, "dp", split_axis=0, concat_axis=1, tiled=True)
+    partial_value = jnp.concatenate(
+        lax.all_to_all(
+            jnp.stack(jnp.split(products, lax.axis_size("dp"), 0), axis=0),
+            axis_name="dp",
+            split_axis=0,
+            concat_axis=0,
+        ),
+        1,
+    )
     summed = lax.psum(partial_value, "tensor")
     hidden_out = (tokens.astype(jnp.float32) + rms_scale(summed, post_gain)).astype(jnp.bfloat16)
     return (hidden_out, new_keys, new_values)

time: 156 us -> 159 us (1.019)
  local copies, waits for them, and re-layouts: 6.5 us -> 11.1 us
    another operation x0 -> x10, local copies, waits for them, and re-layouts: none -> 5.71 us  [per_device(): jnp.stack(jnp.split(products, lax.axis_size('dp'), 0), axis=0)]
where the time goes in v1:
time: 159 us; the launch traced here: 158 us
  waiting for transfers between devices  69 us (43%)
  blocking collectives  31.3 us (20%)
  matrix products  22.1 us (14%)
  between operations  14.3 us (9%)
  local copies, waits for them, and re-layouts  11.1 us (7%)
  other arithmetic  10.5 us (7%)
    psum x1, waiting for transfers between devices, per_device(): summed = lax.psum(partial_value, 'tensor')  35.1 us
    reduce_scatter x1, waiting for transfers between devices, per_device(): lax.psum_scatter(jnp.concatenate([jnp.dot(spread, q_weight, preferred_ele...  33.9 us
    all_to_all x1, blocking collectives, per_device(): lax.all_to_all(normed, 'dp', split_axis=1, concat_axis=0, tiled=True)  11.2 us
    all_to_all x1, blocking collectives, per_device(): lax.all_to_all(jnp.stack(jnp.split(products, lax.axis_size('dp'), 0), axi...  10.8 us
    dot_general x1, matrix products, per_device(): jnp.einsum('bgrd,bjgd->bgrj', grouped, cache_keys, preferred_element_type...  10.4 us
    all_gather x1, blocking collectives, per_device(): lax.all_gather(attended, 'dp', axis=0, tiled=True)  9.27 us
    dot_general x1, matrix products, per_device(): jnp.einsum('bgrj,bjgd->bgrd', weights.astype(jnp.bfloat16), cache_values,...  7.87 us
    another operation x10, local copies, waits for them, and re-layouts, per_device(): jnp.stack(jnp.split(products, lax.axis_size('dp'), 0), axis=0)  5.71 us
  transfers between devices with their start and end apart: 2, of which 2 were waited for; matrix products, arithmetic and copies ran while one was open for 1% of the time, Pallas kernels for 0%

profile of v1, /device:TPU:0, one launch (start us, length us, event | category | flops | bytes accessed | tf_op | source)
XLA Modules:
  0.0 158.3 jit_solution(11721423683232220746)
XLA Ops:
  7.2 1.2 fusion.18
  8.4 1.0 fusion.20
  9.8 11.2 %all_to_all.24 = bf16[16,8,672]{2,0,1:T(8,128)(2,1)S(1)} all-to-all(bf16[16,8,672]{2,0,1:T(8,128)(2,1)S(1)} %copy.34), channel_id=1, replica_groups=mesh['dp'=8,'tensor'=4] {'dp'}, dimensions={1} | all-to-all | bytes 344064 | tf_op jit(solution)/shard_map/all_to_all | solution.py:59
  21.0 1.4 fusion.34
  22.4 1.4 fusion.33
  24.2 1.1 pad_maximum_fusion
  26.8 33.9 %reduce-scatter.2.cloned.1.call-done = f32[16,2048]{1,0:T(8,128)} async-done(((f32[128,2048]{1,0:T(8,128)}), f32[16,2048]{1,0:T(8,128)}) %reduce-scatter.2.cloned.1.call-update) | async-done | bytes 131088 | tf_op jit(solution)/shard_map/reduce_scatter | solution.py:60
  60.7 0.8 slice.46
  61.5 0.8 slice_bitcast_fusion.8
  62.4 0.8 slice.32
  64.1 0.7 multiply_multiply_fusion.1
  65.5 10.4 %fusion.31 = (f32[16,4,2]{2,1,0:T(4,128)S(1)}, f32[16,4,2,1024]{3,2,1,0:T(2,128)S(1)}) fusion(bf16[16,4,2,128]{3,2,1,0:T(2,128)(2,1)S(1)} %fusion.26, pred[16,1024]{1,0:T(8,128)(4,1)S(1)} %iota_compare_fusion, bf16[16,1024,512]{2,1,0:T(8,128)(2,1)} %param.22), kind=kOutput, calls=%fused_computation.67 | convolution fusion | flops 33816448 | bytes 17351168 | tf_op jit(solution)/shard_map/bgrd,bjgd->bgrj/dot_general | solution.py:96
  76.5 7.9 %fusion.12 = bf16[16,4,2,128]{3,2,1,0:T(2,128)(2,1)} fusion(f32[16,4,2,1024]{3,2,1,0:T(2,128)S(1)} %get-tuple-element.20, f32[16,4,2]{2,1,0:T(4,128)S(1)} %get-tuple-element.4, f32[16,4,2]{2,1,0:T(4,128)S(1)} %bitcast.84, f32[16,4,128]{2,1,0:T(4,128)S(1)} %reshape.156, f32[16,4,2]{2,1,0:T(4,128)S(1)} %convert_element_type.58, bf16[16,1024,512]{2,1,0:T(8,128)(2,1)} %param.23), kind=kOutput, calls=%fused_computation.9 | convolution fusion | flops 33882112 | bytes 17368576 | tf_op jit(solution)/shard_map/bgrj,bjgd->bgrd/dot_general | solution.py:104
  84.4 0.8 convert_element_type.62
  85.2 9.3 %all_gather.3 = bf16[128,1024]{1,0:T(8,128)(2,1)S(1)} all-gather(bf16[16,1024]{1,0:T(8,128)(2,1)S(1)} %convert_element_type.62), channel_id=1, replica_groups=mesh['dp'=8,'tensor'=4] {'dp'}, dimensions={0}, use_global_device_ids=true | all-gather | bytes 294912 | tf_op jit(solution)/shard_map/all_gather | solution.py:113
  95.0 1.7 %slice_bitcast_fusion = (f32[1,16,672]{1,2,0:T(8,128)}, f32[1,16,672]{1,2,0:T(8,128)}, f32[1,16,672]{1,2,0:T(8,128)}, f32[1,16,672]{1,2,0:T(8,128)S(1)}, f32[1,1...) fusion(f32[128,672]{0,1:T(8,128)S(1)} %fusion.35), kind=kLoop, calls=%fused_computation.19 | loop fusion | bytes 688128 | tf_op jit(solution)/shard_map/stack | solution.py:119
  96.7 1.1 copy.44
  97.8 1.1 copy.43
  98.9 1.1 copy.42
  100.8 10.8 %all_to_all.25 = f32[8,16,672]{2,1,0:T(8,128)S(1)} all-to-all(f32[8,16,672]{2,1,0:T(8,128)S(1)} %constant_dynamic-update-slice_fusion), channel_id=1, replica_groups=mesh['dp'=8,'tensor'=4] {'dp'}, dimensions={0} | all-to-all | bytes 688128 | tf_op jit(solution)/shard_map/all_to_all | solution.py:118
  111.9 0.9 reshape.155
  113.5 35.1 %all-reduce.2.cloned.1.call-done = f32[16,5376]{1,0:T(8,128)} async-done(((f32[16,5376]{1,0:T(8,128)}), f32[16,5376]{1,0:T(8,128)}) %all-reduce.2.cloned.1.call-update) | async-done | bytes 344080 | tf_op jit(solution)/shard_map/psum | solution.py:126
  148.6 1.1 multiply_reduce_fusion
  149.7 1.8 %fusion.21 = bf16[16,5376]{1,0:T(8,128)(2,1)} fusion(bf16[16,5376]{1,0:T(8,128)(2,1)S(1)} %copy-done.1, f32[16,5376]{1,0:T(8,128)} %all-reduce.2.cloned.1.call-done, f32[5376]{0:T(1024)} %param.25, f32[16]{0:T(128)S(1)} %add_rsqrt_fusion.2), kind=kLoop, calls=%fused_computation.18 | loop fusion | flops 430080 | bytes 709696 | tf_op jit(solution)/shard_map/convert_element_type | solution.py:127
  (55 shorter events, 6.8 us)
Async XLA Ops:
  7.2 16.6 %copy-start = (bf16[672,1024]{1,0:T(8,128)(2,1)S(1)}, bf16[672,1024]{1,0:T(8,128)(2,1)}, u32[]{:S(2)}) copy-start(bf16[672,1024]{1,0:T(8,128)(2,1)} %param.17) | copy-start | bytes 4128772
  7.2 53.6 %reduce-scatter.2.cloned.1.call-start = ((), (), s32[]{:S(2)}) async-start(), calls=%async_computation.3 | async-start | bytes 1179648 | tf_op jit(solution)/shard_map/reduce_scatter | solution.py:60
  25.3 123.3 %all-reduce.2.cloned.1.call-start = ((), (), s32[]{:S(2)}) async-start(), calls=%async_computation.4 | async-start | bytes 688128 | tf_op jit(solution)/shard_map/psum | solution.py:126
  61.5 22.9 %copy-start.3 = (bf16[16,512]{1,0:T(8,128)(2,1)}, bf16[16,512]{1,0:T(8,128)(2,1)S(1)}, u32[]{:S(2)}) copy-start(bf16[16,512]{1,0:T(8,128)(2,1)S(1)} %slice.46) | copy-start | bytes 49156
  65.5 29.0 %copy-start.2 = (bf16[1024,672]{0,1:T(8,128)(2,1)S(1)}, bf16[1024,672]{0,1:T(8,128)(2,1)}, u32[]{:S(2)}) copy-start(bf16[1024,672]{0,1:T(8,128)(2,1)} %param.24) | copy-start | bytes 4128772
  76.5 73.2 %copy-start.1 = (bf16[16,5376]{1,0:T(8,128)(2,1)S(1)}, bf16[16,5376]{1,0:T(8,128)(2,1)}, u32[]{:S(2)}) copy-start(bf16[16,5376]{1,0:T(8,128)(2,1)} %param.13) | copy-start | bytes 516100
Sparse Core Ops, SparseCore 0:
  25.4 35.3 reduce-scatter.1
  112.9 35.6 all-reduce.1

commit v2 on v0

--- a/solution.py
+++ b/solution.py
@@ -8,6 +8,11 @@
 epsilon = 1e-06
 rope_base = 1000000.0
 rope_factor = 8.0
+
+
+def gather_and_add(x, name):
+    pieces = lax.all_gather(x, name)
+    return jnp.sum(pieces, axis=0)
 
 
 def rms_scale(vectors, gain):
@@ -115,7 +120,7 @@
         preferred_element_type=jnp.float32,
     )
     partial_value = lax.all_to_all(products, "dp", split_axis=0, concat_axis=1, tiled=True)
-    summed = lax.psum(partial_value, "tensor")
+    summed = gather_and_add(partial_value, "tensor")
     hidden_out = (tokens.astype(jnp.float32) + rms_scale(summed, post_gain)).astype(jnp.bfloat16)
     return (hidden_out, new_keys, new_values)
 

time: 156 us -> 153 us (0.981)
  waiting for transfers between devices: 69 us -> 66.1 us
    psum x1 -> x0, waiting for transfers between devices: 35.1 us -> none  [per_device(): summed = lax.psum(partial_value, 'tensor')]
    all_gather x0 -> x1, waiting for transfers between devices: none -> 32.2 us  [gather_and_add(): pieces = lax.all_gather(x, name)]
where the time goes in v2:
time: 153 us; the launch traced here: 152 us
  waiting for transfers between devices  66.1 us (43%)
  blocking collectives  31.3 us (20%)
  matrix products  22.2 us (15%)
  between operations  14.2 us (9%)
  other arithmetic  12.1 us (8%)
  local copies, waits for them, and re-layouts  6.5 us (4%)
    reduce_scatter x1, waiting for transfers between devices, per_device(): lax.psum_scatter(jnp.concatenate([jnp.dot(spread, q_weight, preferred_ele...  33.9 us
    all_gather x1, waiting for transfers between devices, gather_and_add(): pieces = lax.all_gather(x, name)  32.2 us
    all_to_all x1, blocking collectives, per_device(): lax.all_to_all(normed, 'dp', split_axis=1, concat_axis=0, tiled=True)  11.2 us
    dot_general x1, matrix products, per_device(): jnp.einsum('bgrd,bjgd->bgrj', grouped, cache_keys, preferred_element_type...  11 us
    all_to_all x1, blocking collectives, per_device(): lax.all_to_all(products, 'dp', split_axis=0, concat_axis=1, tiled=True)  10.8 us
    all_gather x1, blocking collectives, per_device(): lax.all_gather(attended, 'dp', axis=0, tiled=True)  9.25 us
    dot_general x1, matrix products, per_device(): jnp.einsum('bgrj,bjgd->bgrd', weights.astype(jnp.bfloat16), cache_values,...  7.27 us
  transfers between devices with their start and end apart: 2, of which 2 were waited for; matrix products, arithmetic and copies ran while one was open for 1% of the time, Pallas kernels for 0%

profile of v2, /device:TPU:0, one launch (start us, length us, event | category | flops | bytes accessed | tf_op | source)
XLA Modules:
  0.0 152.5 jit_solution(12556330761204786170)
XLA Ops:
  7.2 1.2 fusion.18
  8.4 1.0 fusion.20
  9.8 11.2 %all_to_all.35 = bf16[16,8,672]{2,0,1:T(8,128)(2,1)S(1)} all-to-all(bf16[16,8,672]{2,0,1:T(8,128)(2,1)S(1)} %copy.23), channel_id=1, replica_groups=mesh['dp'=8,'tensor'=4] {'dp'}, dimensions={1} | all-to-all | bytes 344064 | tf_op jit(solution)/shard_map/all_to_all | solution.py:64
  21.4 1.4 fusion.33
  22.8 1.4 fusion.34
  24.2 1.1 pad_maximum_fusion
  25.3 0.7 convert_multiply_fusion.2
  26.0 0.7 iota_compare_fusion
  26.8 33.9 %reduce-scatter.2.cloned.1.call-done = f32[16,2048]{1,0:T(8,128)} async-done(((f32[128,2048]{1,0:T(8,128)}), f32[16,2048]{1,0:T(8,128)}) %reduce-scatter.2.cloned.1.call-update) | async-done | bytes 131088 | tf_op jit(solution)/shard_map/reduce_scatter | solution.py:65
  60.7 0.8 slice.32
  61.6 0.8 slice_bitcast_fusion
  62.6 0.7 multiply_multiply_fusion.1
  63.3 0.7 multiply_multiply_fusion
  64.7 11.0 %fusion.31 = (f32[16,4,2]{2,1,0:T(4,128)}, f32[16,4,2,1024]{3,2,1,0:T(2,128)S(1)}) fusion(bf16[16,4,2,128]{3,2,1,0:T(2,128)(2,1)S(1)} %fusion.26, pred[16,1024]{1,0:T(8,128)(4,1)S(1)} %iota_compare_fusion, bf16[16,1024,512]{2,1,0:T(8,128)(2,1)} %param.22), kind=kOutput, calls=%fused_computation.51 | convolution fusion | flops 33816448 | bytes 17351168 | tf_op jit(solution)/shard_map/bgrd,bjgd->bgrj/dot_general | solution.py:101
  75.7 0.8 fusion.30
  77.2 1.4 slice.46
  78.5 1.3 reshape.152
  80.4 7.3 %fusion.12 = bf16[16,4,2,128]{3,2,1,0:T(2,128)(2,1)S(1)} fusion(f32[16,4,2,1024]{3,2,1,0:T(2,128)S(1)} %get-tuple-element.12, f32[16,4,2]{2,1,0:T(4,128)S(1)} %get-tuple-element.4, f32[16,4,2]{2,1,0:T(4,128)S(1)} %bitcast.70, f32[16,4,128]{2,1,0:T(4,128)} %reshape.152, f32[16,4,2]{2,1,0:T(4,128)} %convert_element_type.58, bf16[16,1024,512]{2,1,0:T(8,128)(2,1)} %param.23), kind=kOutput, calls=%fused_computation.9 | convolution fusion | flops 33882112 | bytes 17368576 | tf_op jit(solution)/shard_map/bgrj,bjgd->bgrd/dot_general | solution.py:109
  87.7 9.2 %all_gather.9 = bf16[128,1024]{1,0:T(8,128)(2,1)S(1)} all-gather(bf16[16,1024]{1,0:T(8,128)(2,1)S(1)} %convert_element_type.62), channel_id=1, replica_groups=mesh['dp'=8,'tensor'=4] {'dp'}, dimensions={0}, use_global_device_ids=true | all-gather | bytes 294912 | tf_op jit(solution)/shard_map/all_gather | solution.py:118
  97.6 10.8 %all_to_all.36 = f32[8,16,672]{2,1,0:T(8,128)S(1)} all-to-all(f32[8,16,672]{2,1,0:T(8,128)S(1)} %bitcast.61), channel_id=1, replica_groups=mesh['dp'=8,'tensor'=4] {'dp'}, dimensions={0} | all-to-all | bytes 688128 | tf_op jit(solution)/shard_map/all_to_all | solution.py:122
  108.6 0.9 all_gather.10
  110.3 32.2 %all-gather.2.cloned.1.call-done = f32[4,16,5376]{2,1,0:T(8,128)} async-done(((f32[1,16,5376]{2,1,0:T(8,128)}), f32[4,16,5376]{2,1,0:T(8,128)}) %all-gather.2.cloned.1.call-update) | async-done | bytes 1376272 | tf_op jit(solution)/shard_map/all_gather | solution.py:14
  142.5 1.5 reduce_sum.58
  144.1 1.5 %fusion.21 = bf16[16,5376]{1,0:T(8,128)(2,1)} fusion(bf16[16,5376]{1,0:T(8,128)(2,1)S(1)} %copy-done.1, f32[16,5376]{1,0:T(8,128)S(1)} %reduce_sum.58, f32[5376]{0:T(1024)} %param.25, f32[16]{0:T(128)S(1)} %add_rsqrt_fusion.2), kind=kLoop, calls=%fused_computation.18 | loop fusion | flops 430080 | bytes 709696 | tf_op jit(solution)/shard_map/convert_element_type | solution.py:124
  (37 shorter events, 4.7 us)
Async XLA Ops:
  7.2 13.9 %copy-start = (bf16[672,1024]{1,0:T(8,128)(2,1)S(1)}, bf16[672,1024]{1,0:T(8,128)(2,1)}, u32[]{:S(2)}) copy-start(bf16[672,1024]{1,0:T(8,128)(2,1)} %param.17) | copy-start | bytes 4128772
  7.2 53.5 %reduce-scatter.2.cloned.1.call-start = ((), (), s32[]{:S(2)}) async-start(), calls=%async_computation.3 | async-start | bytes 1179648 | tf_op jit(solution)/shard_map/reduce_scatter | solution.py:65
  25.3 117.2 %all-gather.2.cloned.1.call-start = ((), (), s32[]{:S(2)}) async-start(), calls=%async_computation.4 | async-start | bytes 1720320 | tf_op jit(solution)/shard_map/all_gather | solution.py:14
  64.7 32.3 %copy-start.2 = (bf16[1024,672]{0,1:T(8,128)(2,1)S(1)}, bf16[1024,672]{0,1:T(8,128)(2,1)}, u32[]{:S(2)}) copy-start(bf16[1024,672]{0,1:T(8,128)(2,1)} %param.24) | copy-start | bytes 4128772
  75.7 68.4 %copy-start.1 = (bf16[16,5376]{1,0:T(8,128)(2,1)S(1)}, bf16[16,5376]{1,0:T(8,128)(2,1)}, u32[]{:S(2)}) copy-start(bf16[16,5376]{1,0:T(8,128)(2,1)} %param.13) | copy-start | bytes 516100
Sparse Core Ops, SparseCore 0:
  25.4 35.3 reduce-scatter.1
  109.7 32.7 all-gather.1
